TPU v7x, 32 devices: a whole 2x2x4 slice. The times are simulated.
32 devices in a mesh: row: 4 (over x, core), col: 4 (over z), layer: 2 (over y).
Axes of the slice: x: 2, y: 2, z: 4, core: 2. Of those that a mesh axis runs over, the one named last changes fastest.
Arguments:
- attn_values: bfloat16 [2048, 8192], P('row', ('layer', 'col')), may hold values from -6 to 6
- out_weight: bfloat16 [8192, 8192], P(('layer', 'row'), 'col'), may hold values from -0.09375 to 0.09375
Outputs:
- projected: bfloat16 [2048, 8192], P('row', ('col', 'layer'))
All inputs are finite; a program needn't handle non-finite values.
Results may differ from a plain program's by a relative error of at most 0.001.
Values may be sent and summed in bfloat16 or wider, within the bound.
A program may use at most 128 MiB of HBM per device.

v0:
```python
import jax
import jax.numpy as jnp
from jax import lax
from jax.sharding import PartitionSpec as P


def partner(x, axis, stride):
    return lax.ppermute(x, axis, [(i, i ^ 1 << stride) for i in range(lax.axis_size(axis))])


def shards(attn_values, out_weight):
    own_half = lax.all_gather(attn_values, "col", axis=1, tiled=True)
    other_part = partner(own_half, "layer", 0)
    first_layer = lax.axis_index("layer") == 0
    lower_half = jnp.where(first_layer, own_half, other_part)
    upper_half = jnp.where(first_layer, other_part, own_half)
    column_pair = lax.all_to_all(out_weight, "layer", split_axis=1, concat_axis=0, tiled=True)
    gathered = lax.all_gather(column_pair, "row", axis=0, tiled=True)
    row_count = lax.axis_size("row")
    depth_rows = out_weight.shape[0]
    stacked = gathered.reshape(row_count, 2, depth_rows, gathered.shape[1])
    weight_lower = stacked[:, 0].reshape(row_count * depth_rows, gathered.shape[1])
    weight_upper = stacked[:, 1].reshape(row_count * depth_rows, gathered.shape[1])
    summed = jnp.dot(lower_half, weight_lower, preferred_element_type=jnp.float32)
    summed = summed + jnp.dot(upper_half, weight_upper, preferred_element_type=jnp.float32)
    projected = summed.astype(jnp.bfloat16)
    return projected


def solution(mesh):
    in_specs = (P("row", ("layer", "col")), P(("layer", "row"), "col"))
    out_specs = P("row", ("col", "layer"))
    return jax.shard_map(shards, mesh=mesh, in_specs=in_specs, out_specs=out_specs, check_vma=False)
```

profile of v0, /device:TPU:0, one launch (start us, length us, event | category | flops | bytes accessed | tf_op | source)
XLA Modules:
  0.0 224.6 jit_solution(15008742448602999398)
XLA Ops:
  6.5 0.0 all-gather.3.cloned.1.call-start
  6.5 0.7 all-gather.3.cloned.1.call-update
  7.3 0.0 all-gather.5.cloned.1.call-start
  7.3 6.5 %copy.3 = bf16[1024,2048]{0,1:T(8,128)(2,1)} copy(bf16[1024,2048]{1,0:T(8,128)(2,1)} %param.3) | data formatting | bytes 8388608 | tf_op args[1]
  13.8 56.3 %all_to_all.19 = bf16[1024,2,1024]{0,2,1:T(8,128)(2,1)} all-to-all(bf16[1024,2,1024]{0,2,1:T(8,128)(2,1)} %bitcast.11), channel_id=1, replica_groups=mesh['row'=4,'col'=4,'layer'=2] {'layer'}, dimensions={1} | all-to-all | bytes 8388608 | tf_op jit(solution)/shard_map/all_to_all | solution.py:17
  70.1 6.3 %copy.4 = bf16[2,1024,1024]{2,1,0:T(8,128)(2,1)} copy(bf16[2,1024,1024]{1,2,0:T(8,128)(2,1)} %bitcast.10) | data formatting | bytes 8388608 | tf_op jit(solution)/shard_map/all_to_all | solution.py:17
  76.3 0.0 all-gather.5.cloned.1.call-update
  76.4 16.0 %all-gather.3.cloned.1.call-done = bf16[512,4096]{1,0:T(8,128)(2,1)} async-done(((bf16[512,1024]{1,0:T(8,128)(2,1)}), bf16[512,4096]{1,0:T(8,128)(2,1)}) %all-gather.3.cloned.1.call-update) | async-done | bytes 4194320 | tf_op jit(solution)/shard_map/all_gather | solution.py:12
  92.4 1.5 collective-permute-start
  93.9 104.5 %all-gather.5.cloned.1.call-done = bf16[8192,1024]{1,0:T(8,128)(2,1)} async-done(((bf16[2048,1024]{1,0:T(8,128)(2,1)}), bf16[8192,1024]{1,0:T(8,128)(2,1)}) %all-gather.5.cloned.1.call-update) | async-done | bytes 16777232 | tf_op jit(solution)/shard_map/all_gather | solution.py:18
  198.4 0.0 copy-start
  198.4 7.0 %fusion.8 = (bf16[4,1,1024,1024]{3,2,1,0:T(8,128)(2,1)S(1)}, bf16[4,1,1024,1024]{3,2,1,0:T(8,128)(2,1)S(1)}) fusion(bf16[4,2,1024,1024]{3,2,1,0:T(8,128)(2,1)} %bitcast.8), kind=kLoop, calls=%fused_computation.7 | loop fusion | bytes 33554432 | tf_op jit(solution)/shard_map/slice | solution.py:22
  205.4 0.0 collective-permute-done
  205.4 0.0 copy-done
  205.4 6.8 %fusion = f32[512,1024]{1,0:T(8,128)S(1)} fusion(bf16[4096,1024]{1,0:T(8,128)(2,1)S(1)} %bitcast.13, bf16[512,4096]{1,0:T(8,128)(2,1)} %collective-permute-done, bf16[512,4096]{1,0:T(8,128)(2,1)S(1)} %copy-done, pred[]{:T(512)S(6)} %eq.3), kind=kOutput, calls=%fused_computation | convolution fusion | flops 4297064448 | bytes 18874368 | tf_op jit(solution)/shard_map/dot_general | solution.py:25
  212.2 5.6 %add_convert_fusion = bf16[512,1024]{1,0:T(8,128)(2,1)} fusion(f32[512,1024]{1,0:T(8,128)S(1)} %fusion, bf16[4096,1024]{1,0:T(8,128)(2,1)S(1)} %bitcast.12, bf16[512,4096]{1,0:T(8,128)(2,1)S(1)} %copy-done, bf16[512,4096]{1,0:T(8,128)(2,1)} %collective-permute-done, pred[]{:T(512)S(6)} %eq.3), kind=kOutput, calls=%fused_computation.6 | convolution fusion | flops 4298113024 | bytes 19922944 | tf_op jit(solution)/shard_map/dot_general | solution.py:24
Async XLA Ops:
  6.5 85.9 %all-gather.3.cloned.1.call-start = ((), (), s32[]{:S(2)}) async-start(), calls=%async_computation.1 | async-start | bytes 5242880 | tf_op jit(solution)/shard_map/all_gather | solution.py:12
  7.3 191.1 %all-gather.5.cloned.1.call-start = ((), (), s32[]{:S(2)}) async-start(), calls=%async_computation.2 | async-start | bytes 20971520 | tf_op jit(solution)/shard_map/all_gather | solution.py:18
  92.4 113.0 %collective-permute-start = (bf16[512,4096]{1,0:T(8,128)(2,1)}, bf16[512,4096]{1,0:T(8,128)(2,1)}, u32[]{:S(2)}, u32[]{:S(2)}) collective-permute-start(bf16[512,4096]{1,0:T(8,128)(2,1)} %all-gather.3.cloned.1.call-done), channel_id=1, source_target_pairs={{0,1},{1,0},{2,3},{3,2},{4,5},{5,4},{6,7},{7,6},{8,9},{9,8},{10,11... | collective-permute-start | bytes 12582920 | tf_op jit(solution)/shard_map/ppermute | solution.py:8
  198.4 7.1 %copy-start = (bf16[512,4096]{1,0:T(8,128)(2,1)S(1)}, bf16[512,4096]{1,0:T(8,128)(2,1)}, u32[]{:S(2)}) copy-start(bf16[512,4096]{1,0:T(8,128)(2,1)} %all-gather.3.cloned.1.call-done) | copy-start | bytes 12582916
Sparse Core Ops, SparseCore 0:
  8.9 83.4 all-gather.2
  93.9 104.3 all-gather.4
where the time goes:
time: 225 us
  waiting for transfers between devices  121 us (54%)
  blocking collectives  56.3 us (25%)
  local copies, waits for them, and re-layouts  19.8 us (9%)
  between operations  13.4 us (6%)
  matrix products  12.4 us (6%)
    all_gather x1, waiting for transfers between devices, shards(): gathered = lax.all_gather(column_pair, 'row', axis=0, tiled=True)  104 us
    all_to_all x1, blocking collectives, shards(): lax.all_to_all(out_weight, 'layer', split_axis=1, concat_axis=0, tiled=True)  56.3 us
    all_gather x1, waiting for transfers between devices, shards(): own_half = lax.all_gather(attn_values, 'col', axis=1, tiled=True)  16 us
    slice x1, local copies, waits for them, and re-layouts, shards(): stacked[:, 0].reshape(row_count * depth_rows, gathered.shape[1])  6.99 us
    dot_general x1, matrix products, shards(): jnp.dot(upper_half, weight_upper, preferred_element_type=jnp.float32)  6.79 us
    unnamed x3, local copies, waits for them, and re-layouts  6.5 us
    all_to_all x1, local copies, waits for them, and re-layouts, shards(): lax.all_to_all(out_weight, 'layer', split_axis=1, concat_axis=0, tiled=True)  6.26 us
    dot_general x1, matrix products, shards(): jnp.dot(lower_half, weight_lower, preferred_element_type=jnp.float32)  5.57 us
  transfers between devices with their start and end apart: 3, of which 2 were waited for; matrix products, arithmetic and copies ran while one was open for 9% of the time, Pallas kernels for 0%

commit v1 on v0

--- a/solution.py
+++ b/solution.py
@@ -14,7 +14,10 @@
     first_layer = lax.axis_index("layer") == 0
     lower_half = jnp.where(first_layer, own_half, other_part)
     upper_half = jnp.where(first_layer, other_part, own_half)
-    column_pair = lax.all_to_all(out_weight, "layer", split_axis=1, concat_axis=0, tiled=True)
+    count = lax.axis_size("layer")
+    pieces = jnp.stack(jnp.split(out_weight, count, axis=1), axis=0)
+    pieces = lax.all_to_all(pieces, "layer", split_axis=0, concat_axis=0)
+    column_pair = jnp.concatenate(pieces, axis=0)
     gathered = lax.all_gather(column_pair, "row", axis=0, tiled=True)
     row_count = lax.axis_size("row")
     depth_rows = out_weight.shape[0]

time: 225 us -> 225 us (level)
  waiting for transfers between devices: 121 us -> 135 us
  local copies, waits for them, and re-layouts: 19.8 us -> 9.7 us
  blocking collectives: 56.3 us -> 52.6 us
    all_gather x1, waiting for transfers between devices: 16 us -> 29.4 us  [shards(): own_half = lax.all_gather(attn_values, 'col', axis=1, tiled=True)]
    unnamed x3 -> x2, local copies, waits for them, and re-layouts: 6.5 us -> 0.04 us
    all_to_all x1 -> x0, local copies, waits for them, and re-layouts: 6.26 us -> none  [shards(): lax.all_to_all(out_weight, 'layer', split_axis=1, concat_axis=0, tiled=True)]
    all_to_all x1, blocking collectives: 56.3 us -> 52.6 us  [shards(): pieces = lax.all_to_all(pieces, 'layer', split_axis=0, concat_axis=0)]
    another operation x0 -> x1, local copies, waits for them, and re-layouts: none -> 2.66 us  [shards(): pieces = jnp.stack(jnp.split(out_weight, count, axis=1), axis=0)]
  transfers between devices with their start and end apart: 3 -> 3, of which waited for: 2 -> 2; matrix products, arithmetic and copies ran while one was open for 9% -> 4% of each run, Pallas kernels for 0% -> 0%
where the time goes in v1:
time: 225 us
  waiting for transfers between devices  135 us (60%)
  blocking collectives  52.6 us (23%)
  between operations  13.4 us (6%)
  matrix products  12.4 us (6%)
  local copies, waits for them, and re-layouts  9.7 us (4%)
    all_gather x1, waiting for transfers between devices, shards(): gathered = lax.all_gather(column_pair, 'row', axis=0, tiled=True)  104 us
    all_to_all x1, blocking collectives, shards(): pieces = lax.all_to_all(pieces, 'layer', split_axis=0, concat_axis=0)  52.6 us
    all_gather x1, waiting for transfers between devices, shards(): own_half = lax.all_gather(attn_values, 'col', axis=1, tiled=True)  29.4 us
    slice x1, local copies, waits for them, and re-layouts, shards(): stacked[:, 0].reshape(row_count * depth_rows, gathered.shape[1])  6.99 us
    dot_general x1, matrix products, shards(): jnp.dot(upper_half, weight_upper, preferred_element_type=jnp.float32)  6.79 us
    dot_general x1, matrix products, shards(): jnp.dot(lower_half, weight_lower, preferred_element_type=jnp.float32)  5.57 us
  transfers between devices with their start and end apart: 3, of which 2 were waited for; matrix products, arithmetic and copies ran while one was open for 4% of the time, Pallas kernels for 0%

profile of v1, /device:TPU:0, one launch (start us, length us, event | category | flops | bytes accessed | tf_op | source)
XLA Modules:
  0.0 224.6 jit_solution(3076637762112578204)
XLA Ops:
  6.5 0.0 all-gather.3.cloned.1.call-start
  6.5 0.7 all-gather.3.cloned.1.call-update
  7.3 0.0 all-gather.5.cloned.1.call-start
  7.3 2.7 %slice_bitcast_fusion.1 = (bf16[1,1024,1024]{2,1,0:T(8,128)(2,1)S(1)}, bf16[1,1024,1024]{2,1,0:T(8,128)(2,1)S(1)}) fusion(bf16[1024,2048]{1,0:T(8,128)(2,1)} %param.3), kind=kLoop, calls=%fused_computation.9 | loop fusion | bytes 8388608 | tf_op jit(solution)/shard_map/stack | solution.py:18
  10.0 0.4 pad_maximum_fusion
  10.4 52.6 %all_to_all.5 = bf16[2,1024,1024]{2,1,0:T(8,128)(2,1)} all-to-all(bf16[2,1024,1024]{2,1,0:T(8,128)(2,1)S(1)} %pad_maximum_fusion), channel_id=1, replica_groups=mesh['row'=4,'col'=4,'layer'=2] {'layer'}, dimensions={0} | all-to-all | bytes 8388608 | tf_op jit(solution)/shard_map/all_to_all | solution.py:19
  63.0 0.0 all-gather.5.cloned.1.call-update
  63.0 29.4 %all-gather.3.cloned.1.call-done = bf16[512,4096]{1,0:T(8,128)(2,1)} async-done(((bf16[512,1024]{1,0:T(8,128)(2,1)}), bf16[512,4096]{1,0:T(8,128)(2,1)}) %all-gather.3.cloned.1.call-update) | async-done | bytes 4194320 | tf_op jit(solution)/shard_map/all_gather | solution.py:12
  92.4 1.5 collective-permute-start
  93.9 104.5 %all-gather.5.cloned.1.call-done = bf16[8192,1024]{1,0:T(8,128)(2,1)} async-done(((bf16[2048,1024]{1,0:T(8,128)(2,1)}), bf16[8192,1024]{1,0:T(8,128)(2,1)}) %all-gather.5.cloned.1.call-update) | async-done | bytes 16777232 | tf_op jit(solution)/shard_map/all_gather | solution.py:21
  198.4 0.0 copy-start
  198.4 7.0 %fusion.8 = (bf16[4,1,1024,1024]{3,2,1,0:T(8,128)(2,1)S(1)}, bf16[4,1,1024,1024]{3,2,1,0:T(8,128)(2,1)S(1)}) fusion(bf16[4,2,1024,1024]{3,2,1,0:T(8,128)(2,1)} %bitcast.10), kind=kLoop, calls=%fused_computation.10 | loop fusion | bytes 33554432 | tf_op jit(solution)/shard_map/slice | solution.py:25
  205.4 0.0 collective-permute-done
  205.4 0.0 copy-done
  205.4 6.8 %fusion = f32[512,1024]{1,0:T(8,128)S(1)} fusion(bf16[4096,1024]{1,0:T(8,128)(2,1)S(1)} %bitcast.13, bf16[512,4096]{1,0:T(8,128)(2,1)} %collective-permute-done, bf16[512,4096]{1,0:T(8,128)(2,1)S(1)} %copy-done, pred[]{:T(512)S(6)} %eq.3), kind=kOutput, calls=%fused_computation.1 | convolution fusion | flops 4297064448 | bytes 18874368 | tf_op jit(solution)/shard_map/dot_general | solution.py:28
  212.2 5.6 %add_convert_fusion = bf16[512,1024]{1,0:T(8,128)(2,1)} fusion(f32[512,1024]{1,0:T(8,128)S(1)} %fusion, bf16[4096,1024]{1,0:T(8,128)(2,1)S(1)} %bitcast.12, bf16[512,4096]{1,0:T(8,128)(2,1)S(1)} %copy-done, bf16[512,4096]{1,0:T(8,128)(2,1)} %collective-permute-done, pred[]{:T(512)S(6)} %eq.3), kind=kOutput, calls=%fused_computation.7 | convolution fusion | flops 4298113024 | bytes 19922944 | tf_op jit(solution)/shard_map/dot_general | solution.py:27
Async XLA Ops:
  6.5 85.9 %all-gather.3.cloned.1.call-start = ((), (), s32[]{:S(2)}) async-start(), calls=%async_computation.1 | async-start | bytes 5242880 | tf_op jit(solution)/shard_map/all_gather | solution.py:12
  7.3 191.1 %all-gather.5.cloned.1.call-start = ((), (), s32[]{:S(2)}) async-start(), calls=%async_computation.2 | async-start | bytes 20971520 | tf_op jit(solution)/shard_map/all_gather | solution.py:21
  92.4 113.0 %collective-permute-start = (bf16[512,4096]{1,0:T(8,128)(2,1)}, bf16[512,4096]{1,0:T(8,128)(2,1)}, u32[]{:S(2)}, u32[]{:S(2)}) collective-permute-start(bf16[512,4096]{1,0:T(8,128)(2,1)} %all-gather.3.cloned.1.call-done), channel_id=1, source_target_pairs={{0,1},{1,0},{2,3},{3,2},{4,5},{5,4},{6,7},{7,6},{8,9},{9,8},{10,11... | collective-permute-start | bytes 12582920 | tf_op jit(solution)/shard_map/ppermute | solution.py:8
  198.4 7.1 %copy-start = (bf16[512,4096]{1,0:T(8,128)(2,1)S(1)}, bf16[512,4096]{1,0:T(8,128)(2,1)}, u32[]{:S(2)}) copy-start(bf16[512,4096]{1,0:T(8,128)(2,1)} %all-gather.3.cloned.1.call-done) | copy-start | bytes 12582916
Sparse Core Ops, SparseCore 0:
  8.9 83.4 all-gather.2
  93.9 104.3 all-gather.4
